TPU v7x, 32 devices: a whole 2x2x4 slice. The times are simulated.
32 devices in a mesh: dp: 16 (over z, y, x), tp: 2 (over core).
Axes of the slice: x: 2, y: 2, z: 4, core: 2. Of those that a mesh axis runs over, the one named last changes fastest.
Arguments:
- tokens: bfloat16 [2048, 4096], P('dp', 'tp'), may hold values from -6 to 6
- norm_gain: float32 [4096], replicated, may hold values from 0.1 to 1.9
- w_query: bfloat16 [4096, 2048], P(None, 'tp'), may hold values from -0.09375 to 0.09375
- w_key: bfloat16 [4096, 512], P(None, 'tp'), may hold values from -0.09375 to 0.09375
- w_value: bfloat16 [4096, 512], P(None, 'tp'), may hold values from -0.09375 to 0.09375
- w_out: bfloat16 [2048, 4096], P('tp'), may hold values from -0.125 to 0.125
- mlp_gain: float32 [4096], replicated, may hold values from 0.1 to 1.9
- w_gate: bfloat16 [4096, 7168], P(None, 'tp'), may hold values from -0.09375 to 0.09375
- w_up: bfloat16 [4096, 7168], P(None, 'tp'), may hold values from -0.09375 to 0.09375
- w_down: bfloat16 [7168, 4096], P('tp'), may hold values from -0.0625 to 0.0625
- kv_pool: bfloat16 [1024, 2, 4, 128, 128], P('dp', None, 'tp'), may hold values from -160 to 160, as said below
- prefix_len: int32 [16], replicated, may hold values from 1024 to 8192, as said below
- page_owner: int32 [16, 64], replicated, may hold values from -1 to 15, as said below
- page_slot: int32 [16, 64], replicated, may hold values from -1 to 63, as said below
- serving: int32 [16], replicated, may hold values from 0 to 15, each once
Outputs:
- context: bfloat16 [2048, 2048], P('dp', 'tp')
- layer_out: bfloat16 [2048, 4096], P('dp', 'tp')
Inputs may be any that keep to these rules, and one draw needn't show every extreme that they name: `prefix_len`: prefix lengths lie between 1024 and 8192; some request has exactly 8192 cached tokens and some exactly 1024. page_owner[r, p] names an index along dp for p < ceil(prefix_len[r] / 128) and is -1 after; no index holds more than 4 pages of one request, and for every request some index holds exactly 4 of its pages. page_slot[r, p] lies in 0 to 63 where page_owner[r, p] is not -1 and is -1 where it is; no two pages share the same holder and slot. serving is a permutation of the requests. `kv_pool`: cached keys and values, each page with an offset of its own.
All inputs are finite; a program needn't handle non-finite values.
Results may differ from a plain program's by a relative error of at most 0.014.
The roundings to bfloat16 on the way count: a program that leaves them out, or rounds other values in their place, can miss the bound.
Values may be sent and summed in bfloat16 or wider, within the bound.
A program may use at most 256 MiB of HBM per device.

v0:
```python
import math

import jax
import jax.numpy as jnp
from jax import lax
from jax.sharding import PartitionSpec as P

EPS = 1e-05
THETA = 500000.0
NEG = -1e30


def rotate(vectors, positions):
    half_dim = vectors.shape[-1] // 2
    freq_index = jnp.arange(half_dim, dtype=jnp.float32)
    inverse = jnp.power(jnp.float32(THETA), -2.0 * freq_index / vectors.shape[-1])
    angles = positions.astype(jnp.float32)[:, None] * inverse[None, :]
    cosine = jnp.cos(angles)[:, None, :]
    sine = jnp.sin(angles)[:, None, :]
    first = vectors[..., :half_dim]
    second = vectors[..., half_dim:]
    return jnp.concatenate(
        [first * cosine - second * sine, second * cosine + first * sine], axis=-1
    )


def attend(queries, keys_all, values_all, length, new_tokens):
    row_count = queries.shape[1]
    prefix_slots = keys_all.shape[1] - new_tokens
    scores = jnp.einsum("hqd,hkd->hqk", queries, keys_all, preferred_element_type=jnp.float32)
    scores = scores / math.sqrt(queries.shape[2])
    row_token = jnp.arange(row_count, dtype=jnp.int32) % new_tokens
    prefix_ok = jnp.arange(prefix_slots, dtype=jnp.int32) < length
    causal = jnp.arange(new_tokens, dtype=jnp.int32)[None, :] <= row_token[:, None]
    allowed = jnp.concatenate(
        [jnp.broadcast_to(prefix_ok[None, :], (row_count, prefix_slots)), causal], axis=1
    )
    scores = jnp.where(allowed[None], scores, NEG)
    highest = jnp.max(scores, axis=-1, keepdims=True)
    expo = jnp.exp(scores - highest)
    weights = (expo / jnp.sum(expo, axis=-1, keepdims=True)).astype(jnp.bfloat16)
    result = jnp.einsum("hqk,hkd->hqd", weights, values_all, preferred_element_type=jnp.float32)
    return result.astype(jnp.bfloat16)


def shards(
    tokens,
    norm_gain,
    w_query,
    w_key,
    w_value,
    w_out,
    mlp_gain,
    w_gate,
    w_up,
    w_down,
    kv_pool,
    prefix_len,
    page_owner,
    page_slot,
    serving,
):
    groups = lax.axis_size("dp")
    device = lax.axis_index("dp")
    tp_rank = lax.axis_index("tp")
    new_tokens = tokens.shape[0]
    share_width = tokens.shape[1]
    model_width = mlp_gain.shape[0]
    pages_max = page_owner.shape[1]
    per_owner = (pages_max + groups - 1) // groups
    page_len = kv_pool.shape[3]
    head_dim = kv_pool.shape[4]
    kv_heads = kv_pool.shape[2]
    q_heads = w_query.shape[1] // head_dim
    shared = q_heads // kv_heads
    group_ids = jnp.arange(groups, dtype=jnp.int32)
    request = jnp.sum(jnp.where(group_ids == device, serving, 0))
    length = jnp.sum(jnp.where(group_ids == request, prefix_len, 0))
    gathered = lax.all_gather(tokens, "tp", axis=1, tiled=True)
    gathered_f32 = gathered.astype(jnp.float32)
    in_scale = lax.rsqrt(jnp.mean(gathered_f32 * gathered_f32, axis=-1, keepdims=True) + EPS)
    normed = (gathered_f32 * in_scale * norm_gain).astype(jnp.bfloat16)
    positions = length + jnp.arange(new_tokens, dtype=jnp.int32)
    queries = rotate(
        jnp.dot(normed, w_query, preferred_element_type=jnp.float32).reshape(
            new_tokens, q_heads, head_dim
        ),
        positions,
    ).astype(jnp.bfloat16)
    new_keys = rotate(
        jnp.dot(normed, w_key, preferred_element_type=jnp.float32).reshape(
            new_tokens, kv_heads, head_dim
        ),
        positions,
    ).astype(jnp.bfloat16)
    new_values = (
        jnp.dot(normed, w_value, preferred_element_type=jnp.float32)
        .astype(jnp.bfloat16)
        .reshape(new_tokens, kv_heads, head_dim)
    )
    owned = (page_owner == device).astype(jnp.int32)
    order_rank = jnp.cumsum(owned, axis=1) - 1
    owned_dest = jnp.take(owned, serving, axis=0)
    rank_dest = jnp.take(order_rank, serving, axis=0)
    slot_dest = jnp.take(page_slot, serving, axis=0)
    choose = jnp.arange(per_owner, dtype=jnp.int32)
    picked = (owned_dest[:, None, :] == 1) & (rank_dest[:, None, :] == choose[None, :, None])
    slot_pick = jnp.sum(jnp.where(picked, slot_dest[:, None, :], 0), axis=2)
    present = jnp.any(picked, axis=2).reshape(-1)
    outbox = jnp.take(kv_pool, slot_pick.reshape(-1), axis=0)
    outbox = jnp.where(present[:, None, None, None, None], outbox, jnp.zeros((), kv_pool.dtype))
    outbox = outbox.reshape((groups, per_owner) + kv_pool.shape[1:])
    incoming = lax.all_to_all(outbox, "dp", split_axis=0, concat_axis=0, tiled=True)
    owner_row = jnp.take(page_owner, request, axis=0)
    page_ids = jnp.arange(pages_max, dtype=jnp.int32)
    earlier = page_ids[None, :] < page_ids[:, None]
    same_owner = owner_row[:, None] == owner_row[None, :]
    row_rank = jnp.sum((earlier & same_owner).astype(jnp.int32), axis=1)
    source = jnp.where(owner_row >= 0, owner_row * per_owner + row_rank, 0)
    inbox = incoming.reshape((groups * per_owner,) + kv_pool.shape[1:])
    prefix_pages = jnp.take(inbox, source, axis=0)
    keys_all = jnp.concatenate(
        [
            prefix_pages[:, 0]
            .transpose(1, 0, 2, 3)
            .reshape(kv_heads, pages_max * page_len, head_dim),
            new_keys.transpose(1, 0, 2),
        ],
        axis=1,
    )
    values_all = jnp.concatenate(
        [
            prefix_pages[:, 1]
            .transpose(1, 0, 2, 3)
            .reshape(kv_heads, pages_max * page_len, head_dim),
            new_values.transpose(1, 0, 2),
        ],
        axis=1,
    )
    stacked = (
        queries.reshape(new_tokens, kv_heads, shared, head_dim)
        .transpose(1, 2, 0, 3)
        .reshape(kv_heads, shared * new_tokens, head_dim)
    )
    attended = attend(stacked, keys_all, values_all, length, new_tokens)
    context = (
        attended.reshape(kv_heads, shared, new_tokens, head_dim)
        .transpose(2, 0, 1, 3)
        .reshape(new_tokens, q_heads * head_dim)
    )
    projected = jnp.dot(context, w_out, preferred_element_type=jnp.float32)
    col_start = tp_rank * share_width
    attn_own = lax.psum_scatter(
        projected.astype(jnp.bfloat16), "tp", scatter_dimension=1, tiled=True
    ).astype(jnp.float32)
    stream_own = (tokens.astype(jnp.float32) + attn_own).astype(jnp.bfloat16)
    own_f32 = stream_own.astype(jnp.float32)
    square_total = lax.psum(jnp.sum(own_f32 * own_f32, axis=-1), "tp")
    gain_own = lax.dynamic_slice_in_dim(mlp_gain, col_start, share_width, 0)
    mid_scale = lax.rsqrt(square_total / model_width + EPS)
    normed_share = (own_f32 * mid_scale[:, None] * gain_own).astype(jnp.bfloat16)
    mlp_in = lax.all_gather(normed_share, "tp", axis=1, tiled=True)
    gate_act = jnp.dot(mlp_in, w_gate, preferred_element_type=jnp.float32)
    up_act = jnp.dot(mlp_in, w_up, preferred_element_type=jnp.float32)
    hidden = (jax.nn.silu(gate_act) * up_act).astype(jnp.bfloat16)
    down_part = jnp.dot(hidden, w_down, preferred_element_type=jnp.float32)
    mlp_own = lax.psum_scatter(
        down_part.astype(jnp.bfloat16), "tp", scatter_dimension=1, tiled=True
    ).astype(jnp.float32)
    layer_out = (stream_own.astype(jnp.float32) + mlp_own).astype(jnp.bfloat16)
    return (context, layer_out)


def solution(mesh):
    in_specs = (
        P("dp", "tp"),
        P(),
        P(None, "tp"),
        P(None, "tp"),
        P(None, "tp"),
        P("tp", None),
        P(),
        P(None, "tp"),
        P(None, "tp"),
        P("tp", None),
        P("dp", None, "tp", None, None),
        P(),
        P(),
        P(),
        P(),
    )
    out_specs = (P("dp", "tp"), P("dp", "tp"))
    return jax.shard_map(shards, mesh=mesh, in_specs=in_specs, out_specs=out_specs, check_vma=False)
```

profile of v0, /device:TPU:0, one launch (start us, length us, event | category | flops | bytes accessed | tf_op | source)
XLA Modules:
  0.0 393.2 jit_solution(11947775346171872055)
XLA Ops:
  13.5 8.9 %gather_fusion.3 = bf16[64,2,2,128,128]{4,3,2,1,0:T(8,128)(2,1)} fusion(bf16[64,2,2,128,128]{4,3,2,1,0:T(8,128)(2,1)} %param.29, s32[1024]{0:T(1024)S(1)} %pad_clamp_fusion.1), kind=kCustom, calls=%fused_computation.1.clone | custom fusion | bytes 16777472 | tf_op jit(solution)/shard_map/jit(_take)/gather | solution.py:110
  22.3 7.6 %select_select_fusion = bf16[64,2,2,128,128]{4,3,2,1,0:T(8,128)(2,1)} fusion(bf16[64,2,2,128,128]{4,3,2,1,0:T(8,128)(2,1)} %gather_fusion.3, pred[64]{0:T(512)(128)(4,1)S(1)} %compare_and_fusion.1, pred[64]{0:T(512)(128)(4,1)S(1)} %broadcast_in_dim.109), kind=kLoop, calls=%fused_computation.12 | loop fusion | flops 8388608 | bytes 16777344 | tf_op jit(solution)/shard_map/jit(_where)/select_n | solution.py:111
  30.0 8.5 %all-to-all-start = ((bf16[16,4,2,2,128,128]{5,4,3,2,1,0:T(8,128)(2,1)}), bf16[16,4,2,2,128,128]{5,4,3,2,1,0:T(8,128)(2,1)}, u32[]{:S(2)}, u32[]{:S(2)}) async-start(bf16[16,4,2,2,128,128]{5,4,3,2,1,0:T(8,128)(2,1)} %bitcast.48), calls=%async_computation | async-start | bytes 16777216 | tf_op jit(solution)/shard_map/all_to_all | solution.py:113
  41.4 3.2 pad_add_fusion
  49.1 2.0 all-gather.3.cloned.1.call-done
  54.4 5.1 %convolution_bitcast_fusion = f32[16,8,8,128]{3,1,2,0:T(8,128)S(1)} fusion(bf16[4096,1024]{1,0:T(8,128)(2,1)} %param.21, bf16[128,4096]{1,0:T(8,128)(2,1)} %all-gather.3.cloned.1.call-done, f32[4096]{0:T(1024)S(1)} %copy-done.7, f32[128]{0:T(128)S(1)} %add_rsqrt_fusion.1), kind=kOutput, calls=%fused_computation.40 | convolution fusion | flops 1075838976 | bytes 9978368 | tf_op jit(solution)/shard_map/dot_general | solution.py:85
  61.2 135.5 %all-to-all-done = bf16[16,4,2,2,128,128]{5,4,3,2,1,0:T(8,128)(2,1)} async-done(((bf16[16,4,2,2,128,128]{5,4,3,2,1,0:T(8,128)(2,1)}), bf16[16,4,2,2,128,128]{5,4,3,2,1,0:T(8,128)(2,1)}, u32[]{:S(2)}, u32[]{:S(2)}) %all-to-all-start) | async-done | bytes 8388640 | tf_op jit(solution)/shard_map/all_to_all | solution.py:113
  196.7 8.9 %gather_fusion.4 = bf16[64,2,2,128,128]{4,3,2,1,0:T(8,128)(2,1)} fusion(bf16[64,2,2,128,128]{4,3,2,1,0:T(8,128)(2,1)} %bitcast.6, s32[1024]{0:T(1024)S(1)} %pad_clamp_fusion), kind=kCustom, calls=%fused_computation.4.clone | custom fusion | bytes 16777472 | tf_op jit(solution)/shard_map/jit(_take)/gather | solution.py:121
  205.6 7.5 %broadcast_select_fusion = bf16[64,2,2,128,128]{4,3,2,1,0:T(8,128)(2,1)} fusion(bf16[64,2,2,128,128]{4,3,2,1,0:T(8,128)(2,1)} %gather_fusion.4, pred[64]{0:T(512)(128)(4,1)S(1)} %get-tuple-element.15), kind=kLoop, calls=%fused_computation.13 | loop fusion | flops 4194304 | bytes 16777280 | tf_op jit(solution)/shard_map/jit(_take)/select_n | solution.py:121
  213.0 3.8 slice_bitcast_fusion.1
  216.8 2.3 copy.38
  219.1 2.3 copy.35
  221.4 17.7 %fusion = (f32[2,512]{1,0:T(2,128)S(1)}, f32[2,512,8320]{2,1,0:T(8,128)}) fusion(pred[512,8320]{1,0:T(8,128)(4,1)} %pad_add_fusion, bf16[2,512,128]{2,1,0:T(8,128)(2,1)S(1)} %bitcast.54, bf16[2,128,128]{2,1,0:T(8,128)(2,1)S(1)} %maximum_bitcast_fusion, bf16[2,8192,128]{2,1,0:T(8,128)(2,1)} %bitcast.51), kind=kOutput, calls=%fused_computation.8 | convolution fusion | flops 2215115776 | bytes 42864640 | tf_op jit(solution)/shard_map/hqd,hkd->hqk/dot_general | solution.py:30
  239.1 16.4 %fusion.1 = f32[2,512]{1,0:T(2,128)S(1)} fusion(f32[2,512,8320]{2,1,0:T(8,128)} %get-tuple-element.32, f32[2,512]{1,0:T(2,128)S(1)} %get-tuple-element.31, pred[512,8320]{1,0:T(8,128)(4,1)} %pad_add_fusion), kind=kLoop, calls=%fused_computation.9 | loop fusion | flops 34077696 | bytes 38346752 | tf_op jit(solution)/shard_map/reduce_sum | solution.py:41
  255.5 17.2 %fusion.19 = bf16[2,512,128]{2,1,0:T(8,128)(2,1)S(1)} fusion(bf16[2,128,128]{2,1,0:T(8,128)(2,1)S(1)} %bitcast.56, bf16[2,8192,128]{2,1,0:T(8,128)(2,1)S(1)} %bitcast.50, f32[2,512,8320]{2,1,0:T(8,128)} %get-tuple-element.32, f32[2,512]{1,0:T(2,128)S(1)} %fusion.1, f32[2,512]{1,0:T(2,128)S(1)} %get-tuple-element.31, pred[512,8320]{1,0:T(8,128)(4,1)} %pad_add_fusion), kind=kOutput, calls=%fused_computation.41 | convolution fusion | flops 2232287232 | bytes 42868736 | tf_op jit(solution)/shard_map/hqk,hkd->hqd/dot_general | solution.py:42
  273.1 5.7 %convolution_convert_fusion.1 = bf16[128,4096]{1,0:T(8,128)(2,1)} fusion(bf16[128,1024]{1,0:T(8,128)(2,1)S(1)} %reshape.158, bf16[1024,4096]{1,0:T(8,128)(2,1)} %param.24), kind=kOutput, calls=%fused_computation.17 | convolution fusion | flops 1074266112 | bytes 9699328 | tf_op jit(solution)/shard_map/dot_general | solution.py:151
  278.9 40.9 %reduce-scatter.3.cloned.1.call-done = bf16[128,2048]{1,0:T(8,128)(2,1)} async-done(((bf16[128,4096]{1,0:T(8,128)(2,1)}), bf16[128,2048]{1,0:T(8,128)(2,1)}) %reduce-scatter.3.cloned.1.call-update) | async-done | bytes 524304 | tf_op jit(solution)/shard_map/reduce_scatter | solution.py:153
  321.1 2.5 psum.7
  323.6 2.0 fusion.25
  325.7 10.3 %all-gather.5.cloned.1.call-done = bf16[128,4096]{1,0:T(8,128)(2,1)} async-done(((bf16[128,2048]{1,0:T(8,128)(2,1)}), bf16[128,4096]{1,0:T(8,128)(2,1)}) %all-gather.5.cloned.1.call-update) | async-done | bytes 1048592 | tf_op jit(solution)/shard_map/all_gather | solution.py:162
  336.0 14.9 %fusion.47 = f32[128,3584]{1,0:T(8,128)} fusion(bf16[128,4096]{1,0:T(8,128)(2,1)} %all-gather.5.cloned.1.call-done, bf16[4096,3584]{1,0:T(8,128)(2,1)} %param.26), kind=kOutput, calls=%fused_computation.105 | convolution fusion | flops 3758096384 | bytes 32243712 | tf_op jit(solution)/shard_map/dot_general | solution.py:163
  350.9 23.9 %convolution_convert_fusion = bf16[128,4096]{1,0:T(8,128)(2,1)} fusion(bf16[3584,4096]{1,0:T(8,128)(2,1)} %param.28, bf16[128,4096]{1,0:T(8,128)(2,1)} %all-gather.5.cloned.1.call-done, bf16[4096,3584]{1,0:T(8,128)(2,1)} %param.27, f32[128,3584]{1,0:T(8,128)} %fusion.47), kind=kOutput, calls=%fused_computation.16 | convolution fusion | flops 7519469568 | bytes 62652416 | tf_op jit(solution)/shard_map/dot_general | solution.py:166
  374.8 9.7 %reduce-scatter.5.cloned.1.call-done = bf16[128,2048]{1,0:T(8,128)(2,1)} async-done(((bf16[128,4096]{1,0:T(8,128)(2,1)}), bf16[128,2048]{1,0:T(8,128)(2,1)}) %reduce-scatter.5.cloned.1.call-update) | async-done | bytes 524304 | tf_op jit(solution)/shard_map/reduce_scatter | solution.py:167
  384.6 2.1 fusion.26
  (81 shorter events, 18.3 us)
Async XLA Ops:
  7.2 45.5 %copy-start = (bf16[4096,256]{1,0:T(8,128)(2,1)S(1)}, bf16[4096,256]{1,0:T(8,128)(2,1)}, u32[]{:S(2)}) copy-start(bf16[4096,256]{1,0:T(8,128)(2,1)} %param.23) | copy-start | bytes 6291460
  29.9 9.3 %copy-start.10 = (s32[16]{0:T(128)S(1)}, s32[16]{0:T(128)}, u32[]{:S(2)}) copy-start(s32[16]{0:T(128)} %param.30) | copy-start | bytes 196
  30.0 22.7 %copy-start.7 = (f32[4096]{0:T(1024)S(1)}, f32[4096]{0:T(1024)}, u32[]{:S(2)}) copy-start(f32[4096]{0:T(1024)} %param.20) | copy-start | bytes 49156
  30.0 166.7 %all-to-all-start = ((bf16[16,4,2,2,128,128]{5,4,3,2,1,0:T(8,128)(2,1)}), bf16[16,4,2,2,128,128]{5,4,3,2,1,0:T(8,128)(2,1)}, u32[]{:S(2)}, u32[]{:S(2)}) async-start(bf16[16,4,2,2,128,128]{5,4,3,2,1,0:T(8,128)(2,1)} %bitcast.48), calls=%async_computation | async-start | bytes 16777216 | tf_op jit(solution)/shard_map/all_to_all | solution.py:113
  38.5 12.7 %all-gather.3.cloned.1.call-start = ((), (), s32[]{:S(2)}) async-start(), calls=%async_computation.3 | async-start | bytes 1572864 | tf_op jit(solution)/shard_map/all_gather | solution.py:79
  39.2 280.6 %reduce-scatter.3.cloned.1.call-start = ((), (), s32[]{:S(2)}) async-start(), calls=%async_computation.4 | async-start | bytes 1572864 | tf_op jit(solution)/shard_map/reduce_scatter | solution.py:153
  54.4 5.6 %copy-start.3 = (bf16[128,4096]{1,0:T(8,128)(2,1)S(1)}, bf16[128,4096]{1,0:T(8,128)(2,1)}, u32[]{:S(2)}) copy-start(bf16[128,4096]{1,0:T(8,128)(2,1)} %all-gather.3.cloned.1.call-done) | copy-start | bytes 3145732
  54.4 5.6 %copy-start.9 = (bf16[4096,256]{1,0:T(8,128)(2,1)S(1)}, bf16[4096,256]{1,0:T(8,128)(2,1)}, u32[]{:S(2)}) copy-start(bf16[4096,256]{1,0:T(8,128)(2,1)} %param.22) | copy-start | bytes 6291460
  239.1 16.4 %copy-start.5 = (bf16[2,64,128,128]{3,2,1,0:T(8,128)(2,1)S(1)}, bf16[2,64,128,128]{3,2,1,0:T(8,128)(2,1)}, u32[]{:S(2)}) copy-start(bf16[2,64,128,128]{3,2,1,0:T(8,128)(2,1)} %copy.38) | copy-start | bytes 12582916
  272.6 6.2 %copy-start.8 = (f32[4096]{0:T(1024)S(1)}, f32[4096]{0:T(1024)}, u32[]{:S(2)}) copy-start(f32[4096]{0:T(1024)} %param.25) | copy-start | bytes 49156
  272.6 47.2 %copy-start.2 = (bf16[128,2048]{1,0:T(8,128)(2,1)S(1)}, bf16[128,2048]{1,0:T(8,128)(2,1)}, u32[]{:S(2)}) copy-start(bf16[128,2048]{1,0:T(8,128)(2,1)} %param.19) | copy-start | bytes 1572868
  273.0 52.6 %copy-start.6 = (bf16[128,1024]{1,0:T(8,128)(2,1)}, bf16[128,1024]{1,0:T(8,128)(2,1)S(1)}, u32[]{:S(2)}) copy-start(bf16[128,1024]{1,0:T(8,128)(2,1)S(1)} %reshape.158) | copy-start | bytes 786436
  278.8 57.2 %all-gather.5.cloned.1.call-start = ((), (), s32[]{:S(2)}) async-start(), calls=%async_computation.5 | async-start | bytes 1572864 | tf_op jit(solution)/shard_map/all_gather | solution.py:162
  325.7 58.9 %reduce-scatter.5.cloned.1.call-start = ((), (), s32[]{:S(2)}) async-start(), calls=%async_computation.6 | async-start | bytes 1572864 | tf_op jit(solution)/shard_map/reduce_scatter | solution.py:167
  350.9 33.6 %copy-start.4 = (bf16[128,2048]{1,0:T(8,128)(2,1)S(1)}, bf16[128,2048]{1,0:T(8,128)(2,1)}, u32[]{:S(2)}) copy-start(bf16[128,2048]{1,0:T(8,128)(2,1)} %reduce-scatter.3.cloned.1.call-done) | copy-start | bytes 1572868
  350.9 35.7 %copy-start.1 = (bf16[4096,256]{1,0:T(8,128)(2,1)S(1)}, bf16[4096,256]{1,0:T(8,128)(2,1)}, u32[]{:S(2)}) copy-start(bf16[4096,256]{1,0:T(8,128)(2,1)} %param.23) | copy-start | bytes 6291460
Sparse Core Ops, SparseCore 0:
  40.8 10.2 all-gather.2
  278.9 40.8 reduce-scatter.2
  325.8 10.1 all-gather.4
  375.0 9.5 reduce-scatter.4
where the time goes:
time: 394 us; the launch traced here: 393 us
  waiting for transfers between devices  199 us (51%)
  matrix products  86.8 us (22%)
  other arithmetic  50.2 us (13%)
  local copies, waits for them, and re-layouts  29.8 us (8%)
  between operations  16.1 us (4%)
  starting transfers between devices  8.68 us (2%)
    all_to_all x1, waiting for transfers between devices, shards(): lax.all_to_all(outbox, 'dp', split_axis=0, concat_axis=0, tiled=True)  135 us
    reduce_scatter x1, waiting for transfers between devices, shards(): lax.psum_scatter(projected.astype(jnp.bfloat16), 'tp', scatter_dimension=...  40.9 us
    dot_general x1, matrix products, shards(): down_part = jnp.dot(hidden, w_down, preferred_element_type=jnp.float32)  23.9 us
    dot_general x1, matrix products, attend(): jnp.einsum('hqd,hkd->hqk', queries, keys_all, preferred_element_type=jnp....  17.7 us
    dot_general x1, matrix products, attend(): jnp.einsum('hqk,hkd->hqd', weights, values_all, preferred_element_type=jn...  17.2 us
    reduce_sum x1, other arithmetic, attend(): jnp.sum(expo, axis=-1, keepdims=True)  16.4 us
    dot_general x1, matrix products, shards(): gate_act = jnp.dot(mlp_in, w_gate, preferred_element_type=jnp.float32)  14.9 us
    all_gather x1, waiting for transfers between devices, shards(): mlp_in = lax.all_gather(normed_share, 'tp', axis=1, tiled=True)  10.3 us
  transfers between devices with their start and end apart: 5, of which 5 were waited for; matrix products, arithmetic and copies ran while one was open for 5% of the time, Pallas kernels for 0%

commit v1 on v0

v1 whole, which is shorter than its diff:
```python
import functools
import math

import jax
import jax.numpy as jnp
from jax import lax
from jax.experimental import pallas as pl
from jax.experimental.pallas import tpu as pltpu
from jax.sharding import PartitionSpec as P

EPS = 1e-05
THETA = 500000.0
NEG = -1e30
MESH = pl.DeviceIdType.MESH
VMEM = pltpu.VMEM


def rotate(vectors, positions):
    half_dim = vectors.shape[-1] // 2
    freq_index = jnp.arange(half_dim, dtype=jnp.float32)
    inverse = jnp.power(jnp.float32(THETA), -2.0 * freq_index / vectors.shape[-1])
    angles = positions.astype(jnp.float32)[:, None] * inverse[None, :]
    cosine = jnp.cos(angles)[:, None, :]
    sine = jnp.sin(angles)[:, None, :]
    first = vectors[..., :half_dim]
    second = vectors[..., half_dim:]
    return jnp.concatenate(
        [first * cosine - second * sine, second * cosine + first * sine], axis=-1
    )


def bit_orders(levels):
    down = list(range(levels - 1, -1, -1))
    swapped = down[:-2] + [down[-1], down[-2]]
    low_first = [0, 1] + list(range(levels - 1, 1, -1))
    return [down, swapped, low_first]


def head_groups(heads):
    first = (heads + 2) // 3
    second = (heads - first + 1) // 2
    sizes = [first, second, heads - first - second]
    starts = [0, first, first + second]
    return list(zip(starts, sizes))


def span(bits):
    masks = [0]
    for bit in bits:
        masks = masks + [mask | (1 << bit) for mask in masks]
    return masks


def flipped(me, mask):
    out = me
    bit = 0
    while (1 << bit) <= mask:
        if mask & (1 << bit):
            out = out + (1 - 2 * (lax.rem(me // (1 << bit), 2))) * (1 << bit)
        bit += 1
    return out


def greet(levels, me):
    barrier = pltpu.get_barrier_semaphore()
    for bit in range(levels):
        pl.semaphore_signal(
            barrier, inc=1, device_id={"dp": flipped(me, 1 << bit)}, device_id_type=MESH
        )
    pl.semaphore_wait(barrier, levels)


def gather_kernel(levels, q_ref, out_ref, send_sem, recv_sem, own_sem):
    me = lax.axis_index("dp")
    greet(levels, me)
    groups = head_groups(q_ref.shape[0])
    orders = bit_orders(levels)
    sends = []
    own = pltpu.make_async_copy(q_ref, out_ref.at[me], own_sem)
    own.start()

    def copy_of(piece, mask, bit):
        start, size = groups[piece]
        block = flipped(me, mask)
        heads = pl.ds(start, size)
        key = mask | (1 << bit)
        source = q_ref.at[heads] if mask == 0 else out_ref.at[block, heads]
        return pltpu.make_async_remote_copy(
            src_ref=source,
            dst_ref=out_ref.at[block, heads],
            send_sem=send_sem.at[piece, key],
            recv_sem=recv_sem.at[piece, key],
            device_id={"dp": flipped(me, 1 << bit)},
            device_id_type=MESH,
        )

    def wait_arrival(piece, mask):
        start, size = groups[piece]
        landed = out_ref.at[flipped(me, mask), pl.ds(start, size)]
        pltpu.make_async_copy(landed, landed, recv_sem.at[piece, mask]).wait()

    for level in range(levels):
        for index in range(1 << level):
            for piece in range(3):
                if groups[piece][1] == 0:
                    continue
                order = orders[piece]
                mask = span(order[:level])[index]
                if mask and index >= (1 << (level - 1)):
                    wait_arrival(piece, mask)
                copy = copy_of(piece, mask, order[level])
                copy.start()
                sends.append(copy)
    for piece in range(3):
        if groups[piece][1]:
            for mask in span(orders[piece])[1 << (levels - 1) :]:
                wait_arrival(piece, mask)
    for copy in sends:
        copy.wait_send()
    own.wait()


def attend_kernel(
    per_owner, slot_ref, valid_ref, q_ref, kv_ref, nk_ref, nv_ref, part_ref, stat_ref
):
    me = lax.axis_index("dp")
    total, heads, rows, width = q_ref.shape
    kv_heads = kv_ref.shape[2]
    page = kv_ref.shape[3]
    shared = heads // kv_heads
    scale = 1.0 / math.sqrt(width)
    stat_row = lax.broadcasted_iota(jnp.int32, (8, rows), 0)

    def scores_of(keys, group, kv_head):
        queries = q_ref[group, kv_head * shared : (kv_head + 1) * shared]
        queries = queries.reshape(shared * rows, width)
        return (
            lax.dot_general(
                keys, queries, (((1,), (1,)), ((), ())), preferred_element_type=jnp.float32
            )
            * scale
        )

    def summed(scores, values):
        highest = jnp.max(scores, axis=0, keepdims=True)
        expo = jnp.exp(scores - highest)
        total_of = jnp.sum(expo, axis=0, keepdims=True)
        part = lax.dot_general(
            values,
            expo.astype(jnp.bfloat16),
            (((0,), (0,)), ((), ())),
            preferred_element_type=jnp.float32,
        )
        return highest, total_of, part

    def stats(highest, total_of):
        return jnp.where(stat_row < 4, highest, total_of)

    def one_group(group, carry):
        held = valid_ref[group, 0] > 0

        @pl.when(held)
        def _():
            row = lax.broadcasted_iota(jnp.int32, (page, 1), 0)
            ok = jnp.concatenate(
                [row < valid_ref[group, k] for k in range(per_owner)], axis=0
            )
            for kv_head in range(kv_heads):
                keys = jnp.concatenate(
                    [kv_ref[slot_ref[group, k], 0, kv_head] for k in range(per_owner)], axis=0
                )
                values = jnp.concatenate(
                    [kv_ref[slot_ref[group, k], 1, kv_head] for k in range(per_owner)], axis=0
                )
                scores = jnp.where(ok, scores_of(keys, group, kv_head), NEG)
                highest, total_of, part = summed(scores, values)
                for j in range(shared):
                    lanes = slice(j * rows, (j + 1) * rows)
                    part_ref[group, kv_head * shared + j] = part[:, lanes].astype(jnp.bfloat16)
                    stat_ref[group, kv_head * shared + j] = stats(
                        highest[:, lanes], total_of[:, lanes]
                    )

        @pl.when(jnp.logical_not(held))
        def _():
            for head in range(heads):
                part_ref[group, head] = jnp.zeros((width, rows), jnp.bfloat16)
                stat_ref[group, head] = jnp.where(stat_row < 4, NEG, 0.0)

        return carry

    lax.fori_loop(0, total, one_group, 0)

    key_row = lax.broadcasted_iota(jnp.int32, (rows, shared * rows), 0)
    token = lax.rem(lax.broadcasted_iota(jnp.int32, (rows, shared * rows), 1), rows)
    for kv_head in range(kv_heads):
        scores = jnp.where(key_row <= token, scores_of(nk_ref[kv_head], me, kv_head), NEG)
        highest, total_of, part = summed(scores, nv_ref[kv_head])
        for j in range(shared):
            head = kv_head * shared + j
            lanes = slice(j * rows, (j + 1) * rows)
            before = stat_ref[me, head]
            top, count, summed_part = merge(
                before[0:1],
                before[4:5],
                part_ref[me, head].astype(jnp.float32),
                highest[:, lanes],
                total_of[:, lanes],
                part[:, lanes],
            )
            part_ref[me, head] = summed_part.astype(jnp.bfloat16)
            stat_ref[me, head] = stats(top, count)


def merge(top_a, count_a, part_a, top_b, count_b, part_b):
    top = jnp.maximum(top_a, top_b)
    factor_a = jnp.exp(top_a - top)
    factor_b = jnp.exp(top_b - top)
    return (
        top,
        count_a * factor_a + count_b * factor_b,
        part_a * factor_a + part_b * factor_b,
    )


def home_kernel(
    levels, part_ref, stat_ref, out_ref, part_box, stat_box, part_send, part_recv, stat_send, stat_recv
):
    me = lax.axis_index("dp")
    greet(levels, me)
    heads, width, rows = part_ref.shape[1:]
    groups = head_groups(heads)
    orders = [order[::-1] for order in bit_orders(levels)]
    stat_row = lax.broadcasted_iota(jnp.int32, (8, rows), 0)
    sends = []
    where = {}

    def held(piece, mask):
        if (piece, mask) in where:
            key = where[piece, mask]
            return part_box.at[key], stat_box.at[key]
        block = flipped(me, mask)
        return part_ref.at[block], stat_ref.at[block]

    def send(piece, level, mask):
        order = orders[piece]
        bit = 1 << order[level]
        cut = pl.ds(*groups[piece])
        part, stat = held(piece, mask)
        for source, box, out_sem, in_sem in (
            (part, part_box, part_send, part_recv),
            (stat, stat_box, stat_send, stat_recv),
        ):
            copy = pltpu.make_async_remote_copy(
                src_ref=source.at[cut],
                dst_ref=box.at[mask, cut],
                send_sem=out_sem.at[piece, mask],
                recv_sem=in_sem.at[piece, mask],
                device_id={"dp": flipped(me, bit)},
                device_id_type=MESH,
            )
            copy.start()
            sends.append(copy)

    def take(piece, level, mask):
        order = orders[piece]
        key = mask | (1 << order[level])
        start, size = groups[piece]
        cut = pl.ds(start, size)
        part, stat = held(piece, mask)
        for box, in_sem in ((part_box, part_recv), (stat_box, stat_recv)):
            landed = box.at[key, cut]
            pltpu.make_async_copy(landed, landed, in_sem.at[piece, key]).wait()
        last = level == levels - 1

        def one_head(head):
            mine = stat[head]
            came = stat_box[key, head]
            top, count, merged = merge(
                mine[0:1],
                mine[4:5],
                part[head].astype(jnp.float32),
                came[0:1],
                came[4:5],
                part_box[key, head].astype(jnp.float32),
            )
            return top, count, merged

        if last:
            for head in range(start, start + size):
                _, count, merged = one_head(head)
                out_ref[:, head * width : (head + 1) * width] = (merged / count).T.astype(
                    out_ref.dtype
                )
        else:

            def body(head, carry):
                top, count, merged = one_head(head)
                part_box[key, head] = merged.astype(jnp.bfloat16)
                stat_box[key, head] = jnp.where(stat_row < 4, top, count)
                return carry

            lax.fori_loop(start, start + size, body, 0)
            where[piece, mask] = key

    live = [piece for piece in range(3) if groups[piece][1]]
    for index in range(1 << (levels - 1)):
        for piece in live:
            order = orders[piece]
            send(piece, 0, span(order[:0:-1])[index] | (1 << order[0]))
    for level in range(levels):
        if level == levels - 1:
            for piece in live:
                take(piece, level, 0)
            break
        for forward in (True, False):
            for index in range(1 << (levels - 2 - level)):
                for piece in live:
                    order = orders[piece]
                    mask = span(order[: level + 1 : -1])[index]
                    if forward:
                        mask = mask | (1 << order[level + 1])
                    take(piece, level, mask)
                    if forward:
                        send(piece, level + 1, mask)
    for copy in sends:
        copy.wait_send()


def attention(queries, new_keys, new_values, kv_pool, slot_pick, valid, groups, per_owner):
    heads, rows, width = queries.shape
    levels = groups.bit_length() - 1
    vmem = pl.BlockSpec(memory_space=VMEM)
    smem = pl.BlockSpec(memory_space=pltpu.SMEM)
    dma = pltpu.SemaphoreType.DMA
    all_queries = pl.pallas_call(
        functools.partial(gather_kernel, levels),
        out_shape=jax.ShapeDtypeStruct((groups, heads, rows, width), jnp.bfloat16),
        in_specs=[vmem],
        out_specs=vmem,
        scratch_shapes=[dma((3, groups)), dma((3, groups)), dma],
        compiler_params=pltpu.CompilerParams(collective_id=0, has_side_effects=True),
        name="query_gather",
    )(queries)
    parts, stats = pl.pallas_call(
        functools.partial(attend_kernel, per_owner),
        out_shape=(
            jax.ShapeDtypeStruct((groups, heads, width, rows), jnp.bfloat16),
            jax.ShapeDtypeStruct((groups, heads, 8, rows), jnp.float32),
        ),
        in_specs=[smem, smem, vmem, vmem, vmem, vmem],
        out_specs=(vmem, vmem),
        name="page_attend",
    )(slot_pick, valid, all_queries, kv_pool, new_keys, new_values)
    return pl.pallas_call(
        functools.partial(home_kernel, levels),
        out_shape=jax.ShapeDtypeStruct((rows, heads * width), jnp.bfloat16),
        in_specs=[vmem, vmem],
        out_specs=vmem,
        scratch_shapes=[
            pltpu.VMEM((groups, heads, width, rows), jnp.bfloat16),
            pltpu.VMEM((groups, heads, 8, rows), jnp.float32),
            dma((3, groups)),
            dma((3, groups)),
            dma((3, groups)),
            dma((3, groups)),
        ],
        compiler_params=pltpu.CompilerParams(collective_id=1, has_side_effects=True),
        name="context_home",
    )(parts, stats)


def shards(
    tokens,
    norm_gain,
    w_query,
    w_key,
    w_value,
    w_out,
    mlp_gain,
    w_gate,
    w_up,
    w_down,
    kv_pool,
    prefix_len,
    page_owner,
    page_slot,
    serving,
):
    groups = lax.axis_size("dp")
    device = lax.axis_index("dp")
    tp_rank = lax.axis_index("tp")
    new_tokens = tokens.shape[0]
    share_width = tokens.shape[1]
    model_width = mlp_gain.shape[0]
    pages_max = page_owner.shape[1]
    per_owner = (pages_max + groups - 1) // groups
    page_len = kv_pool.shape[3]
    head_dim = kv_pool.shape[4]
    kv_heads = kv_pool.shape[2]
    q_heads = w_query.shape[1] // head_dim
    group_ids = jnp.arange(groups, dtype=jnp.int32)
    request = jnp.sum(jnp.where(group_ids == device, serving, 0))
    length = jnp.sum(jnp.where(group_ids == request, prefix_len, 0))
    gathered = lax.all_gather(tokens, "tp", axis=1, tiled=True)
    gathered_f32 = gathered.astype(jnp.float32)
    in_scale = lax.rsqrt(jnp.mean(gathered_f32 * gathered_f32, axis=-1, keepdims=True) + EPS)
    normed = (gathered_f32 * in_scale * norm_gain).astype(jnp.bfloat16)
    positions = length + jnp.arange(new_tokens, dtype=jnp.int32)
    queries = rotate(
        jnp.dot(normed, w_query, preferred_element_type=jnp.float32).reshape(
            new_tokens, q_heads, head_dim
        ),
        positions,
    ).astype(jnp.bfloat16)
    new_keys = rotate(
        jnp.dot(normed, w_key, preferred_element_type=jnp.float32).reshape(
            new_tokens, kv_heads, head_dim
        ),
        positions,
    ).astype(jnp.bfloat16)
    new_values = (
        jnp.dot(normed, w_value, preferred_element_type=jnp.float32)
        .astype(jnp.bfloat16)
        .reshape(new_tokens, kv_heads, head_dim)
    )
    owner_dest = jnp.take(page_owner, serving, axis=0)
    slot_dest = jnp.take(page_slot, serving, axis=0)
    length_dest = jnp.take(prefix_len, serving)
    page_ids = jnp.arange(pages_max, dtype=jnp.int32)
    owned = owner_dest == device
    rank = jnp.cumsum(owned.astype(jnp.int32), axis=1) - 1
    valid_dest = jnp.clip(length_dest[:, None] - page_ids[None, :] * page_len, 0, page_len)
    choose = jnp.arange(per_owner, dtype=jnp.int32)
    picked = owned[:, None, :] & (rank[:, None, :] == choose[None, :, None])
    slot_pick = jnp.sum(jnp.where(picked, slot_dest[:, None, :], 0), axis=2)
    valid = jnp.sum(jnp.where(picked, valid_dest[:, None, :], 0), axis=2)
    context = attention(
        queries.transpose(1, 0, 2),
        new_keys.transpose(1, 0, 2),
        new_values.transpose(1, 0, 2),
        kv_pool,
        slot_pick,
        valid,
        groups,
        per_owner,
    )
    projected = jnp.dot(context, w_out, preferred_element_type=jnp.float32)
    col_start = tp_rank * share_width
    attn_own = lax.psum_scatter(
        projected.astype(jnp.bfloat16), "tp", scatter_dimension=1, tiled=True
    ).astype(jnp.float32)
    stream_own = (tokens.astype(jnp.float32) + attn_own).astype(jnp.bfloat16)
    own_f32 = stream_own.astype(jnp.float32)
    square_total = lax.psum(jnp.sum(own_f32 * own_f32, axis=-1), "tp")
    gain_own = lax.dynamic_slice_in_dim(mlp_gain, col_start, share_width, 0)
    mid_scale = lax.rsqrt(square_total / model_width + EPS)
    normed_share = (own_f32 * mid_scale[:, None] * gain_own).astype(jnp.bfloat16)
    mlp_in = lax.all_gather(normed_share, "tp", axis=1, tiled=True)
    gate_act = jnp.dot(mlp_in, w_gate, preferred_element_type=jnp.float32)
    up_act = jnp.dot(mlp_in, w_up, preferred_element_type=jnp.float32)
    hidden = (jax.nn.silu(gate_act) * up_act).astype(jnp.bfloat16)
    down_part = jnp.dot(hidden, w_down, preferred_element_type=jnp.float32)
    mlp_own = lax.psum_scatter(
        down_part.astype(jnp.bfloat16), "tp", scatter_dimension=1, tiled=True
    ).astype(jnp.float32)
    layer_out = (stream_own.astype(jnp.float32) + mlp_own).astype(jnp.bfloat16)
    return (context, layer_out)


def solution(mesh):
    in_specs = (
        P("dp", "tp"),
        P(),
        P(None, "tp"),
        P(None, "tp"),
        P(None, "tp"),
        P("tp", None),
        P(),
        P(None, "tp"),
        P(None, "tp"),
        P("tp", None),
        P("dp", None, "tp", None, None),
        P(),
        P(),
        P(),
        P(),
    )
    out_specs = (P("dp", "tp"), P("dp", "tp"))
    return jax.shard_map(shards, mesh=mesh, in_specs=in_specs, out_specs=out_specs, check_vma=False)
```

time: 394 us -> 245 us (0.62)
  waiting for transfers between devices: 199 us -> 30.6 us
  Pallas kernels: 0 us -> 119 us
  other arithmetic: 50.2 us -> 14.2 us
  matrix products: 86.8 us -> 55.1 us
  local copies, waits for them, and re-layouts: 29.8 us -> 7.46 us
  starting transfers between devices: 8.68 us -> 0.16 us
    all_to_all x1 -> x0, waiting for transfers between devices: 135 us -> none  [shards(): lax.all_to_all(outbox, 'dp', split_axis=0, concat_axis=0, tiled=True)]
    pallas_call x0 -> x3, Pallas kernels: none -> 119 us  [the longest x1 51.6 us: attention(): pl.pallas_call(functools.partial(home_kernel, levels), out_shape=jax.Shap...]
    dot_general x2 -> x0, matrix products: 34.8 us -> none  [the longest x1 17.7 us: attend(): jnp.einsum('hqd,hkd->hqk', queries, keys_all, preferred_element_type=jnp....]
    reduce_scatter x1, waiting for transfers between devices: 40.9 us -> 7.24 us  [shards(): lax.psum_scatter(projected.astype(jnp.bfloat16), 'tp', scatter_dimension=...]
    reduce_sum x4 -> x1, other arithmetic: 18 us -> 0.22 us  [shards(): valid = jnp.sum(jnp.where(picked, valid_dest[:, None, :], 0), axis=2)]
    gather x4 -> x2, local copies, waits for them, and re-layouts: 18.9 us -> 2.58 us  [the longest x1 1.31 us: shards(): length_dest = jnp.take(prefix_len, serving)]
    select_n x6 -> x2, other arithmetic: 15.8 us -> 1.96 us  [the longest x1 1.3 us: shards(): length_dest = jnp.take(prefix_len, serving)]
    transpose x4 -> x0, local copies, waits for them, and re-layouts: 8.58 us -> none  [the longest x2 6.08 us: shards(): keys_all = jnp.concatenate([prefix_pages[:, 0].transpose(1, 0, 2, 3).resh...]
  transfers between devices with their start and end apart: 5 -> 4, of which waited for: 5 -> 4; matrix products, arithmetic and copies ran while one was open for 5% -> 4% of each run, Pallas kernels for 0% -> 0%
where the time goes in v1:
time: 245 us; the launch traced here: 243 us
  Pallas kernels  119 us (49%)
  matrix products  55.1 us (22%)
  waiting for transfers between devices  30.6 us (12%)
  other arithmetic  14.2 us (6%)
  between operations  14 us (6%)
  local copies, waits for them, and re-layouts  7.46 us (3%)
  blocking collectives  2.64 us (1%)
    pallas_call x1, Pallas kernels, attention(): pl.pallas_call(functools.partial(home_kernel, levels), out_shape=jax.Shap...  51.6 us
    pallas_call x1, Pallas kernels, attention(): pl.pallas_call(functools.partial(gather_kernel, levels), out_shape=jax.Sh...  47.2 us
    dot_general x1, matrix products, shards(): down_part = jnp.dot(hidden, w_down, preferred_element_type=jnp.float32)  24.2 us
    pallas_call x1, Pallas kernels, attention(): pl.pallas_call(functools.partial(attend_kernel, per_owner), out_shape=(ja...  20.2 us
    dot_general x1, matrix products, shards(): gate_act = jnp.dot(mlp_in, w_gate, preferred_element_type=jnp.float32)  14.9 us
    all_gather x1, waiting for transfers between devices, shards(): mlp_in = lax.all_gather(normed_share, 'tp', axis=1, tiled=True)  10.3 us
    reduce_scatter x1, waiting for transfers between devices, shards(): lax.psum_scatter(down_part.astype(jnp.bfloat16), 'tp', scatter_dimension=...  9.7 us
    reduce_scatter x1, waiting for transfers between devices, shards(): lax.psum_scatter(projected.astype(jnp.bfloat16), 'tp', scatter_dimension=...  7.24 us
  transfers between devices with their start and end apart: 4, of which 4 were waited for; matrix products, arithmetic and copies ran while one was open for 4% of the time, Pallas kernels for 0%

profile of v1, /device:TPU:0, one launch (start us, length us, event | category | flops | bytes accessed | tf_op | source)
XLA Modules:
  0.0 243.3 jit_solution(7558489195757865561)
XLA Ops:
  8.6 1.3 gather_fusion
  10.0 1.3 gather_fusion.1
  11.2 1.3 broadcast_select_fusion.1
  12.8 1.3 gather_fusion.2
  15.8 1.9 fusion.16
  18.7 2.7 %all-gather.3.cloned.1.call-done = bf16[128,4096]{1,0:T(8,128)(2,1)} async-done(((bf16[128,2048]{1,0:T(8,128)(2,1)}), bf16[128,4096]{1,0:T(8,128)(2,1)}) %all-gather.3.cloned.1.call-update) | async-done | bytes 1048592 | tf_op jit(solution)/shard_map/all_gather | solution.py:405
  21.3 1.5 fusion.1
  22.9 7.1 %fusion.21 = f32[128,1024]{0,1:T(8,128)S(1)} fusion(bf16[4096,1024]{1,0:T(8,128)(2,1)} %param.19, bf16[128,4096]{1,0:T(8,128)(2,1)} %all-gather.3.cloned.1.call-done, f32[4096]{0:T(1024)S(1)} %copy-done.6, f32[128]{0:T(128)S(1)} %add_rsqrt_fusion.1), kind=kOutput, calls=%fused_computation.58 | convolution fusion | flops 1075838976 | bytes 9978368 | tf_op jit(solution)/shard_map/dot_general | solution.py:411
  30.6 0.9 maximum_bitcast_fusion.q_ref
  31.5 47.2 %query_gather.1.q_ref = bf16[16,8,128,128]{3,2,1,0:T(8,128)(2,1)} custom-call(bf16[8,128,128]{2,1,0:T(8,128)(2,1)} %maximum_bitcast_fusion.q_ref), custom_call_target="tpu_custom_call" | custom-call | tf_op jit(solution)/shard_map/query_gather/pallas_call | solution.py:336
  78.8 1.0 fusion.19
  80.0 2.1 convolution_convert_fusion.2
  83.7 20.2 %page_attend.1 = (bf16[16,8,128,128]{3,2,1,0:T(8,128)(2,1)}, f32[16,8,8,128]{3,2,1,0:T(8,128)}) custom-call(s32[16,4]{1,0:T(8,128)} %copy.33.slot_ref, s32[16,4]{1,0:T(8,128)} %copy.34.valid_ref, bf16[16,8,128,128]{3,2,1,0:T(8,128)(2,1)} %query_gather.1.q_ref, bf16[64,2,2,128,128]{4,3,2,1,0:T(8,128)(2,1)} %kv_ref.1, ...), custom_call_target="tpu_custom_call" | custom-call | tf_op jit(solution)/shard_map/page_attend/pallas_call | solution.py:345
  103.9 51.6 %context_home.1 = bf16[128,1024]{1,0:T(8,128)(2,1)} custom-call(bf16[16,8,128,128]{3,2,1,0:T(8,128)(2,1)} %get-tuple-element.5.part_ref, f32[16,8,8,128]{3,2,1,0:T(8,128)} %get-tuple-element.6.stat_ref), custom_call_target="tpu_custom_call" | custom-call | tf_op jit(solution)/shard_map/context_home/pallas_call | solution.py:355
  155.6 5.8 %convolution_convert_fusion.1 = bf16[128,4096]{1,0:T(8,128)(2,1)} fusion(bf16[128,1024]{1,0:T(8,128)(2,1)} %context_home.1, bf16[1024,4096]{1,0:T(8,128)(2,1)} %param.22), kind=kOutput, calls=%fused_computation.6 | convolution fusion | flops 1074266112 | bytes 9699328 | tf_op jit(solution)/shard_map/dot_general | solution.py:448
  161.5 7.2 %reduce-scatter.3.cloned.1.call-done = bf16[128,2048]{1,0:T(8,128)(2,1)} async-done(((bf16[128,4096]{1,0:T(8,128)(2,1)}), bf16[128,2048]{1,0:T(8,128)(2,1)}) %reduce-scatter.3.cloned.1.call-update) | async-done | bytes 524304 | tf_op jit(solution)/shard_map/reduce_scatter | solution.py:450
  168.7 1.3 fusion.9
  170.0 2.6 %psum.7 = f32[128]{0:T(128)S(1)} all-reduce(f32[128]{0:T(128)S(1)} %fusion.9), channel_id=1, replica_groups=mesh['dp'=16,'tp'=2] {'tp'}, use_global_device_ids=true, to_apply=%region_8.10 | all-reduce | flops 128 | bytes 1024 | tf_op jit(solution)/shard_map/psum | solution.py:455
  172.7 2.0 fusion.11
  174.8 10.3 %all-gather.5.cloned.1.call-done = bf16[128,4096]{1,0:T(8,128)(2,1)} async-done(((bf16[128,2048]{1,0:T(8,128)(2,1)}), bf16[128,4096]{1,0:T(8,128)(2,1)}) %all-gather.5.cloned.1.call-update) | async-done | bytes 1048592 | tf_op jit(solution)/shard_map/all_gather | solution.py:459
  185.1 14.9 %fusion.26 = f32[128,3584]{1,0:T(8,128)} fusion(bf16[128,4096]{1,0:T(8,128)(2,1)} %all-gather.5.cloned.1.call-done, bf16[4096,3584]{1,0:T(8,128)(2,1)} %param.24), kind=kOutput, calls=%fused_computation.62 | convolution fusion | flops 3758096384 | bytes 32243712 | tf_op jit(solution)/shard_map/dot_general | solution.py:460
  200.0 24.2 %convolution_convert_fusion = bf16[128,4096]{1,0:T(8,128)(2,1)} fusion(bf16[3584,4096]{1,0:T(8,128)(2,1)} %param.26, bf16[128,4096]{1,0:T(8,128)(2,1)} %all-gather.5.cloned.1.call-done, bf16[4096,3584]{1,0:T(8,128)(2,1)} %param.25, f32[128,3584]{1,0:T(8,128)} %fusion.26), kind=kOutput, calls=%fused_computation.5 | convolution fusion | flops 7519469568 | bytes 62652416 | tf_op jit(solution)/shard_map/dot_general | solution.py:463
  224.3 9.7 %reduce-scatter.5.cloned.1.call-done = bf16[128,2048]{1,0:T(8,128)(2,1)} async-done(((bf16[128,4096]{1,0:T(8,128)(2,1)}), bf16[128,2048]{1,0:T(8,128)(2,1)}) %reduce-scatter.5.cloned.1.call-update) | async-done | bytes 524304 | tf_op jit(solution)/shard_map/reduce_scatter | solution.py:464
  234.0 2.1 fusion.12
  (56 shorter events, 7.7 us)
Async XLA Ops:
  7.2 71.6 %copy-start = (bf16[4096,256]{1,0:T(8,128)(2,1)S(1)}, bf16[4096,256]{1,0:T(8,128)(2,1)}, u32[]{:S(2)}) copy-start(bf16[4096,256]{1,0:T(8,128)(2,1)} %param.20) | copy-start | bytes 6291460
  7.2 15.7 %copy-start.6 = (f32[4096]{0:T(1024)S(1)}, f32[4096]{0:T(1024)}, u32[]{:S(2)}) copy-start(f32[4096]{0:T(1024)} %param.18) | copy-start | bytes 49156
  7.2 14.1 %all-gather.3.cloned.1.call-start = ((), (), s32[]{:S(2)}) async-start(), calls=%async_computation.2 | async-start | bytes 1572864 | tf_op jit(solution)/shard_map/all_gather | solution.py:405
  7.9 160.8 %reduce-scatter.3.cloned.1.call-start = ((), (), s32[]{:S(2)}) async-start(), calls=%async_computation.3 | async-start | bytes 1572864 | tf_op jit(solution)/shard_map/reduce_scatter | solution.py:450
  22.9 7.1 %copy-start.8 = (f32[128]{0:T(128)}, f32[128]{0:T(128)S(1)}, u32[]{:S(2)}) copy-start(f32[128]{0:T(128)S(1)} %add_rsqrt_fusion.1) | copy-start | bytes 1540
  31.5 47.3 %copy-start.4 = (bf16[128,4096]{1,0:T(8,128)(2,1)S(1)}, bf16[128,4096]{1,0:T(8,128)(2,1)}, u32[]{:S(2)}) copy-start(bf16[128,4096]{1,0:T(8,128)(2,1)} %all-gather.3.cloned.1.call-done) | copy-start | bytes 3145732
  31.5 47.3 %copy-start.9 = (f32[128]{0:T(128)S(1)}, f32[128]{0:T(128)}, u32[]{:S(2)}) copy-start(f32[128]{0:T(128)} %copy-done.8) | copy-start | bytes 1540
  155.6 5.9 %copy-start.7 = (f32[4096]{0:T(1024)S(1)}, f32[4096]{0:T(1024)}, u32[]{:S(2)}) copy-start(f32[4096]{0:T(1024)} %param.23) | copy-start | bytes 49156
  155.6 13.2 %copy-start.2 = (bf16[128,2048]{1,0:T(8,128)(2,1)S(1)}, bf16[128,2048]{1,0:T(8,128)(2,1)}, u32[]{:S(2)}) copy-start(bf16[128,2048]{1,0:T(8,128)(2,1)} %param.17) | copy-start | bytes 1572868
  161.4 23.7 %all-gather.5.cloned.1.call-start = ((), (), s32[]{:S(2)}) async-start(), calls=%async_computation.4 | async-start | bytes 1572864 | tf_op jit(solution)/shard_map/all_gather | solution.py:459
  174.7 59.2 %reduce-scatter.5.cloned.1.call-start = ((), (), s32[]{:S(2)}) async-start(), calls=%async_computation.5 | async-start | bytes 1572864 | tf_op jit(solution)/shard_map/reduce_scatter | solution.py:464
  200.0 34.0 %copy-start.3 = (bf16[128,2048]{1,0:T(8,128)(2,1)S(1)}, bf16[128,2048]{1,0:T(8,128)(2,1)}, u32[]{:S(2)}) copy-start(bf16[128,2048]{1,0:T(8,128)(2,1)} %reduce-scatter.3.cloned.1.call-done) | copy-start | bytes 1572868
  200.0 36.7 %copy-start.1 = (bf16[4096,256]{1,0:T(8,128)(2,1)S(1)}, bf16[4096,256]{1,0:T(8,128)(2,1)}, u32[]{:S(2)}) copy-start(bf16[4096,256]{1,0:T(8,128)(2,1)} %param.20) | copy-start | bytes 6291460
  224.2 11.8 %copy-start.5 = (bf16[128,1024]{1,0:T(8,128)(2,1)S(1)}, bf16[128,1024]{1,0:T(8,128)(2,1)}, u32[]{:S(2)}) copy-start(bf16[128,1024]{1,0:T(8,128)(2,1)} %context_home.1) | copy-start | bytes 786436
Sparse Core Ops, SparseCore 0:
  9.5 11.7 all-gather.2
  161.5 7.1 reduce-scatter.2
  174.9 10.2 all-gather.4
  224.4 9.5 reduce-scatter.4
